TPU v7x, 32 devices: a whole 2x2x4 slice. The times are simulated.
32 devices in a mesh: row: 8 (over y, x, core), col: 4 (over z).
Axes of the slice: x: 2, y: 2, z: 4, core: 2. Of those that a mesh axis runs over, the one named last changes fastest.
Arguments:
- queries: bfloat16 [8, 128, 4096], P(None, 'row', 'col'), may hold values from -13 to 13, as said below
- key_cache: bfloat16 [8, 16384, 1024], P(None, ('row', 'col')), may hold values from -13 to 13
- value_cache: bfloat16 [8, 16384, 1024], P(None, ('row', 'col')), may hold values from -6 to 6
- key_table: bfloat16 [1024, 1024], replicated, may hold values from -24 to 24
- value_table: bfloat16 [1024, 1024], replicated, may hold values from -6 to 6
- lengths: int32 [8], replicated, may hold values from 2048 to 16384
- token_ids: int32 [8, 128], P(None, 'row'), may hold values from 0 to 1023
Outputs:
- attended: bfloat16 [8, 128, 4096], P(None, 'row', 'col')
Inputs may be any that keep to these rules, and one draw needn't show every extreme that they name: `queries`: entries of the query array lie in the stated range.
All inputs are finite; a program needn't handle non-finite values.
Results may differ from a plain program's by a relative error of at most 0.006.
Values may be sent and summed in bfloat16 or wider, within the bound.
A program may use at most 192 MiB of HBM per device.

v0:
```python
import jax
import jax.numpy as jnp
from jax import lax
from jax.sharding import PartitionSpec as P

HQ = 32
KH = 8
HD = 128


def cache_partials(whole, key_cache, value_cache, lengths, offset):
    users, beams, width = whole.shape
    positions = key_cache.shape[1]
    group = HQ // KH
    scale = HD ** (-0.5)

    def one_user(items):
        q_user, k_user, v_user, limit = items
        q_heads = q_user.reshape(beams, KH, group, HD)
        k_heads = k_user.reshape(positions, KH, HD)
        v_heads = v_user.reshape(positions, KH, HD)
        s = (
            jnp.einsum("wkgd,lkd->kwgl", q_heads, k_heads, preferred_element_type=jnp.float32)
            * scale
        )
        live = offset + jnp.arange(positions, dtype=jnp.int32) < limit
        s = jnp.where(live, s, -1e30)
        peak = jnp.max(s, axis=-1)
        weight = jnp.where(live, jnp.exp(s - peak[..., None]), 0.0)
        total = jnp.sum(weight, axis=-1)
        numer = jnp.einsum(
            "kwgl,lkd->wkgd",
            weight.astype(jnp.bfloat16),
            v_heads,
            preferred_element_type=jnp.float32,
        )
        peak = jnp.transpose(peak, (1, 0, 2)).reshape(beams, HQ)
        total = jnp.transpose(total, (1, 0, 2)).reshape(beams, HQ)
        return (numer.reshape(beams, width), peak, total)

    return lax.map(one_user, (whole, key_cache, value_cache, lengths))


def body(queries, key_cache, value_cache, key_table, value_table, lengths, token_ids):
    users, beam_part, width_part = queries.shape
    heads_part = width_part // HD
    scale = HD ** (-0.5)
    row_at = lax.axis_index("row")
    col_at = lax.axis_index("col")
    whole = lax.all_gather(queries, "col", axis=2, tiled=True)
    whole = lax.all_gather(whole, "row", axis=1, tiled=True)
    offset = (row_at * lax.axis_size("col") + col_at) * key_cache.shape[1]
    numer_part, peak_part, total_part = cache_partials(
        whole, key_cache, value_cache, lengths, offset
    )
    peak_all = lax.pmax(peak_part, ("row", "col"))
    factor = jnp.exp(peak_part - peak_all)
    weighted = (numer_part.reshape(users, -1, HQ, HD) * factor[..., None]).reshape(
        users, -1, HQ * HD
    )
    mass = total_part * factor

    def local_part(array, per_head):
        picked = lax.dynamic_slice_in_dim(array, row_at * beam_part, beam_part, 1)
        return lax.dynamic_slice_in_dim(
            picked, col_at * heads_part * per_head, heads_part * per_head, 2
        )

    numer, total = lax.psum((weighted, mass), ("row", "col"))
    numer = local_part(numer, HD)
    total = local_part(total, 1)
    peak = local_part(peak_all, 1)
    codes = jnp.arange(key_table.shape[0], dtype=jnp.int32)
    onehot = (token_ids[..., None] == codes).astype(jnp.bfloat16)
    own_keys = jnp.einsum("uwv,vc->uwc", onehot, key_table, preferred_element_type=jnp.float32)
    own_values = jnp.einsum("uwv,vc->uwc", onehot, value_table, preferred_element_type=jnp.float32)
    group = HQ // KH
    own_keys = jnp.repeat(own_keys.reshape(users, beam_part, KH, HD), group, axis=2)
    own_values = jnp.repeat(own_values.reshape(users, beam_part, KH, HD), group, axis=2)
    own_keys = lax.dynamic_slice_in_dim(own_keys, col_at * heads_part, heads_part, 2)
    own_values = lax.dynamic_slice_in_dim(own_values, col_at * heads_part, heads_part, 2)
    q_local = queries.astype(jnp.float32).reshape(users, beam_part, heads_part, HD)
    own_score = jnp.sum(q_local * own_keys, axis=-1) * scale
    final_peak = jnp.maximum(peak, own_score)
    carried = jnp.exp(peak - final_peak)
    fresh = jnp.exp(own_score - final_peak)
    numer = (
        numer.reshape(users, beam_part, heads_part, HD) * carried[..., None]
        + fresh[..., None] * own_values
    )
    total = total * carried + fresh
    result = numer / total[..., None]
    return result.reshape(users, beam_part, width_part).astype(jnp.bfloat16)


def solution(mesh):
    return jax.shard_map(
        body,
        mesh=mesh,
        in_specs=(
            P(None, "row", "col"),
            P(None, ("row", "col"), None),
            P(None, ("row", "col"), None),
            P(),
            P(),
            P(),
            P(None, "row"),
        ),
        out_specs=P(None, "row", "col"),
        check_vma=False,
    )
```

profile of v0, /device:TPU:0, one launch (start us, length us, event | category | flops | bytes accessed | tf_op | source)
XLA Modules:
  0.0 730.9 jit_solution(4568035272929321944)
XLA Ops:
  6.5 1.9 copy.35
  8.6 31.1 %all-gather.3.cloned.1.call-done = bf16[8,16,4096]{2,0,1:T(8,128)(2,1)} async-done(((bf16[8,16,1024]{2,0,1:T(8,128)(2,1)}), bf16[8,16,4096]{2,0,1:T(8,128)(2,1)}) %all-gather.3.cloned.1.call-update) | async-done | bytes 1048592 | tf_op jit(solution)/shard_map/all_gather | solution.py:50
  39.8 55.4 %all-gather.5.cloned.1.call-done = bf16[8,128,4096]{2,0,1:T(8,128)(2,1)} async-done(((bf16[8,16,4096]{2,0,1:T(8,128)(2,1)}), bf16[8,128,4096]{2,0,1:T(8,128)(2,1)}) %all-gather.5.cloned.1.call-update) | async-done | bytes 8388624 | tf_op jit(solution)/shard_map/all_gather | solution.py:51
  95.2 12.5 %copy.37 = bf16[8,128,4096]{1,2,0:T(8,128)(2,1)} copy(bf16[8,128,4096]{2,0,1:T(8,128)(2,1)} %all-gather.5.cloned.1.call-done) | data formatting | bytes 16777216 | tf_op jit(solution)/shard_map/while | solution.py:41
  107.7 186.9 %while.14 = (s32[]{:T(128)}, f32[8,128,4096]{1,2,0:T(8,128)}, f32[8,128,32]{1,2,0:T(8,128)}, f32[8,128,32]{1,2,0:T(8,128)S(1)}, bf16[8,512,1024]{2,1,0:T(8,128)(...) while((s32[]{:T(128)}, f32[8,128,4096]{1,2,0:T(8,128)}, ...), condition=%wide.region_3.4_spmd, body=%wide.region_0.3_spmd.sunk | while | flops 1100997632 | bytes 78777504 | solution.py:41
  110.3 1.4 copy.58
  112.9 2.8 fusion.35
  115.8 3.2 copy-done.1
  119.0 2.3 fusion.37
  123.3 1.4 copy.57
  124.6 5.0 fusion.36
  129.6 1.5 constant_dynamic-update-slice_fusion.2
  133.6 1.4 copy.58
  136.3 2.8 fusion.35
  139.1 3.2 copy-done.1
  142.4 2.3 fusion.37
  146.6 1.4 copy.57
  148.0 5.0 fusion.36
  152.9 1.5 constant_dynamic-update-slice_fusion.2
  157.0 1.4 copy.58
  159.6 2.8 fusion.35
  162.5 3.2 copy-done.1
  165.7 2.3 fusion.37
  170.0 1.4 copy.57
  171.3 5.0 fusion.36
  176.3 1.5 constant_dynamic-update-slice_fusion.2
  180.3 1.4 copy.58
  183.0 2.8 fusion.35
  185.8 3.2 copy-done.1
  189.1 2.3 fusion.37
  193.3 1.4 copy.57
  194.7 5.0 fusion.36
  199.6 1.5 constant_dynamic-update-slice_fusion.2
  203.7 1.4 copy.58
  206.4 2.8 fusion.35
  209.2 3.2 copy-done.1
  212.4 2.3 fusion.37
  218.1 5.0 fusion.36
  223.0 1.5 constant_dynamic-update-slice_fusion.2
  227.1 1.4 copy.58
  229.7 2.8 fusion.35
  232.6 3.2 copy-done.1
  235.8 2.3 fusion.37
  241.4 5.0 fusion.36
  246.4 1.5 constant_dynamic-update-slice_fusion.2
  250.5 1.4 copy.58
  253.1 2.8 fusion.35
  256.0 3.2 copy-done.1
  259.2 2.3 fusion.37
  264.8 5.0 fusion.36
  269.8 1.5 constant_dynamic-update-slice_fusion.2
  273.8 1.4 copy.58
  276.5 2.8 fusion.35
  279.3 3.2 copy-done.1
  282.6 2.3 fusion.37
  288.2 5.0 fusion.36
  293.1 1.4 constant_dynamic-update-slice_fusion.2
  294.7 124.8 %all-reduce.4.cloned.1.call-done = f32[8,128,32]{1,2,0:T(8,128)} async-done(((f32[8,128,32]{1,2,0:T(8,128)}), f32[8,128,32]{1,2,0:T(8,128)}) %all-reduce.4.cloned.1.call-update) | async-done | bytes 131088 | tf_op jit(solution)/shard_map/pmax | solution.py:56
  419.4 1.7 fusion.20
  421.1 11.3 %bitcast_multiply_fusion = f32[8,128,4096]{1,2,0:T(8,128)} fusion(f32[8,128,4096]{1,2,0:T(8,128)} %get-tuple-element.54, f32[8,128,32]{1,2,0:T(8,128)S(1)} %get-tuple-element.117), kind=kLoop, calls=%fused_computation.17 | loop fusion | flops 4194304 | bytes 33685504 | tf_op jit(solution)/shard_map/mul | solution.py:58
  434.6 2.1 fusion.9
  436.8 276.3 %all-reduce.6.cloned.1.call-done = (f32[8,128,4096]{1,2,0:T(8,128)}, f32[8,128,32]{1,2,0:T(8,128)}) async-done(((f32[8,128,4096]{1,2,0:T(8,128)}, f32[8,128,32]{1,2,0:T(8,128)}), (f32[8,128,4096]{1,2,0:T(8,128)}, f32[8,128,32]{1,2,0:T(8,128)})) %all-reduce.6.cloned.1.call-update) | async-done | bytes 16908304 | tf_op jit(solution)/shard_map/psum | solution.py:69
  714.4 5.3 constant_dynamic-slice_fusion.3
  719.7 2.8 copy.49
  (93 shorter events, 57.1 us)
Async XLA Ops:
  6.5 425.9 %copy-start = (bf16[1024,1024]{1,0:T(8,128)(2,1)S(1)}, bf16[1024,1024]{1,0:T(8,128)(2,1)}, u32[]{:S(2)}) copy-start(bf16[1024,1024]{1,0:T(8,128)(2,1)} %param.12) | copy-start | bytes 6291460
  6.5 33.1 %all-gather.3.cloned.1.call-start = ((), (), s32[]{:S(2)}) async-start(), calls=%async_computation | async-start | bytes 1310720 | tf_op jit(solution)/shard_map/all_gather | solution.py:50
  8.5 86.7 %all-gather.5.cloned.1.call-start = ((), (), s32[]{:S(2)}) async-start(), calls=%async_computation.1 | async-start | bytes 9437184 | tf_op jit(solution)/shard_map/all_gather | solution.py:51
  39.7 379.7 %all-reduce.4.cloned.1.call-start = ((), (), s32[]{:S(2)}) async-start(), calls=%async_computation.2 | async-start | bytes 262144 | tf_op jit(solution)/shard_map/pmax | solution.py:56
  39.8 67.9 %copy-start.4 = (s32[8]{0:T(128)S(1)}, s32[8]{0:T(128)}, u32[]{:S(2)}) copy-start(s32[8]{0:T(128)} %param.14) | copy-start | bytes 100
  115.8 3.2 copy-start.1
  139.1 3.2 copy-start.1
  162.5 3.2 copy-start.1
  185.8 3.2 copy-start.1
  209.2 3.2 copy-start.1
  232.6 3.2 copy-start.1
  256.0 3.2 copy-start.1
  279.3 3.2 copy-start.1
  294.6 418.6 %all-reduce.6.cloned.1.call-start = ((), (), s32[]{:S(2)}) async-start(), calls=%async_computation.3 | async-start | bytes 33816576 | tf_op jit(solution)/shard_map/psum | solution.py:69
  432.4 0.7 copy-start.3
  432.4 1.3 copy-start.2
Sparse Core Ops, SparseCore 0:
  8.9 30.6 all-gather.2
  41.5 53.6 all-gather.4
  294.7 124.6 all-reduce.3
  432.5 280.6 all-reduce.5
where the time goes:
time: 733 us; the launch traced here: 731 us
  waiting for transfers between devices  488 us (67%)
  local copies, waits for them, and re-layouts  126 us (17%)
  matrix products  65 us (9%)
  other arithmetic  38.3 us (5%)
  between operations  13.3 us (2%)
    psum x1, waiting for transfers between devices, body(): numer, total = lax.psum((weighted, mass), ('row', 'col'))  276 us
    pmax x1, waiting for transfers between devices, body(): peak_all = lax.pmax(peak_part, ('row', 'col'))  125 us
    dynamic_slice x48, local copies, waits for them, and re-layouts, cache_partials(): return lax.map(one_user, (whole, key_cache, value_cache, lengths))  57.9 us
    all_gather x1, waiting for transfers between devices, body(): whole = lax.all_gather(whole, 'row', axis=1, tiled=True)  55.4 us
    dot_general x8, matrix products, one_user(): jnp.einsum('kwgl,lkd->wkgd', weight.astype(jnp.bfloat16), v_heads, prefer...  39.7 us
    all_gather x1, waiting for transfers between devices, body(): whole = lax.all_gather(queries, 'col', axis=2, tiled=True)  31.1 us
    while x16, local copies, waits for them, and re-layouts  25.8 us
    dot_general x8, matrix products, one_user(): jnp.einsum('wkgd,lkd->kwgl', q_heads, k_heads, preferred_element_type=jnp...  22.7 us
  transfers between devices with their start and end apart: 4, of which 4 were waited for; matrix products, arithmetic and copies ran while one was open for 1% of the time, Pallas kernels for 0%

commit v1 on v0

--- a/solution.py
+++ b/solution.py
@@ -6,6 +6,11 @@
 HQ = 32
 KH = 8
 HD = 128
+
+
+def one_after_other(x, axis_one, axis_two):
+    inner = lax.psum(x, axis_one)
+    return lax.psum(inner, axis_two)
 
 
 def cache_partials(whole, key_cache, value_cache, lengths, offset):
@@ -66,7 +71,7 @@
             picked, col_at * heads_part * per_head, heads_part * per_head, 2
         )
 
-    numer, total = lax.psum((weighted, mass), ("row", "col"))
+    numer, total = one_after_other((weighted, mass), "col", "row")
     numer = local_part(numer, HD)
     total = local_part(total, 1)
     peak = local_part(peak_all, 1)

time: 733 us -> 1240 us (1.69)
  waiting for transfers between devices: 488 us -> 993 us
    psum x1 -> x2, waiting for transfers between devices: 276 us -> 782 us  [the longest x1 565 us: one_after_other(): inner = lax.psum(x, axis_one)]
  transfers between devices with their start and end apart: 4 -> 5, of which waited for: 4 -> 5; matrix products, arithmetic and copies ran while one was open for 1% -> 0% of each run, Pallas kernels for 0% -> 0%
where the time goes in v1:
time: 1240 us
  waiting for transfers between devices  993 us (80%)
  local copies, waits for them, and re-layouts  126 us (10%)
  matrix products  65 us (5%)
  other arithmetic  38.9 us (3%)
  between operations  13.3 us (1%)
    psum x1, waiting for transfers between devices, one_after_other(): inner = lax.psum(x, axis_one)  565 us
    psum x1, waiting for transfers between devices, one_after_other(): return lax.psum(inner, axis_two)  217 us
    pmax x1, waiting for transfers between devices, body(): peak_all = lax.pmax(peak_part, ('row', 'col'))  125 us
    dynamic_slice x48, local copies, waits for them, and re-layouts, cache_partials(): return lax.map(one_user, (whole, key_cache, value_cache, lengths))  58.2 us
    all_gather x1, waiting for transfers between devices, body(): whole = lax.all_gather(whole, 'row', axis=1, tiled=True)  55.4 us
    dot_general x8, matrix products, one_user(): jnp.einsum('kwgl,lkd->wkgd', weight.astype(jnp.bfloat16), v_heads, prefer...  39.7 us
    all_gather x1, waiting for transfers between devices, body(): whole = lax.all_gather(queries, 'col', axis=2, tiled=True)  31.1 us
    while x16, local copies, waits for them, and re-layouts  25.7 us
  transfers between devices with their start and end apart: 5, of which 5 were waited for; matrix products, arithmetic and copies ran while one was open for 0% of the time, Pallas kernels for 0%

profile of v1, /device:TPU:0, one launch (start us, length us, event | category | flops | bytes accessed | tf_op | source)
XLA Modules:
  0.0 1237.1 jit_solution(2894487895881263465)
XLA Ops:
  6.5 1.9 copy.35
  8.6 31.1 %all-gather.3.cloned.1.call-done = bf16[8,16,4096]{2,0,1:T(8,128)(2,1)} async-done(((bf16[8,16,1024]{2,0,1:T(8,128)(2,1)}), bf16[8,16,4096]{2,0,1:T(8,128)(2,1)}) %all-gather.3.cloned.1.call-update) | async-done | bytes 1048592 | tf_op jit(solution)/shard_map/all_gather | solution.py:55
  39.8 55.4 %all-gather.5.cloned.1.call-done = bf16[8,128,4096]{2,0,1:T(8,128)(2,1)} async-done(((bf16[8,16,4096]{2,0,1:T(8,128)(2,1)}), bf16[8,128,4096]{2,0,1:T(8,128)(2,1)}) %all-gather.5.cloned.1.call-update) | async-done | bytes 8388624 | tf_op jit(solution)/shard_map/all_gather | solution.py:56
  95.2 12.5 %copy.37 = bf16[8,128,4096]{1,2,0:T(8,128)(2,1)} copy(bf16[8,128,4096]{2,0,1:T(8,128)(2,1)} %all-gather.5.cloned.1.call-done) | data formatting | bytes 16777216 | tf_op jit(solution)/shard_map/while | solution.py:46
  107.7 187.6 %while.14 = (s32[]{:T(128)}, f32[8,128,4096]{1,2,0:T(8,128)}, f32[8,128,32]{1,2,0:T(8,128)}, f32[8,128,32]{1,2,0:T(8,128)S(1)}, bf16[8,512,1024]{2,1,0:T(8,128)(...) while((s32[]{:T(128)}, f32[8,128,4096]{1,2,0:T(8,128)}, ...), condition=%wide.region_3.4_spmd, body=%wide.region_0.3_spmd.sunk | while | flops 1100997632 | bytes 78777504 | solution.py:46
  110.3 1.4 copy.58
  113.0 2.8 fusion.35
  115.9 3.2 copy-done.1
  119.1 2.3 fusion.37
  123.3 1.4 copy.57
  124.7 5.0 fusion.36
  129.7 1.5 constant_dynamic-update-slice_fusion.2
  133.8 1.4 copy.58
  136.5 2.8 fusion.35
  139.3 3.2 copy-done.1
  142.5 2.3 fusion.37
  148.1 5.0 fusion.36
  153.1 1.5 constant_dynamic-update-slice_fusion.2
  157.2 1.4 copy.58
  159.9 2.8 fusion.35
  162.7 3.2 copy-done.1
  166.0 2.3 fusion.37
  171.6 5.0 fusion.36
  176.5 1.5 constant_dynamic-update-slice_fusion.2
  180.7 1.4 copy.58
  183.3 2.8 fusion.35
  186.2 3.2 copy-done.1
  189.4 2.3 fusion.37
  193.7 1.4 copy.57
  195.0 5.0 fusion.36
  200.0 1.5 constant_dynamic-update-slice_fusion.2
  204.1 1.4 copy.58
  206.8 2.8 fusion.35
  209.6 3.2 copy-done.1
  212.9 2.3 fusion.37
  218.5 5.0 fusion.36
  223.4 1.5 constant_dynamic-update-slice_fusion.2
  227.6 1.4 copy.58
  230.3 2.8 fusion.35
  233.1 3.2 copy-done.1
  236.4 2.3 fusion.37
  240.6 1.4 copy.57
  242.0 5.0 fusion.36
  246.9 1.5 constant_dynamic-update-slice_fusion.2
  251.1 1.4 copy.58
  253.7 2.8 fusion.35
  256.6 3.2 copy-done.1
  259.8 2.3 fusion.37
  265.4 5.0 fusion.36
  270.4 1.5 constant_dynamic-update-slice_fusion.2
  274.5 1.4 copy.58
  277.2 2.8 fusion.35
  280.0 3.2 copy-done.1
  283.2 2.3 fusion.37
  288.8 5.0 fusion.36
  293.8 1.4 constant_dynamic-update-slice_fusion.2
  295.3 124.8 %all-reduce.6.cloned.1.call-done = f32[8,128,32]{1,2,0:T(8,128)} async-done(((f32[8,128,32]{1,2,0:T(8,128)}), f32[8,128,32]{1,2,0:T(8,128)}) %all-reduce.6.cloned.1.call-update) | async-done | bytes 131088 | tf_op jit(solution)/shard_map/pmax | solution.py:61
  420.1 1.7 fusion.20
  421.7 11.3 bitcast_multiply_fusion
  433.1 565.2 %all-reduce.10.cloned.1.call-done = (f32[8,128,4096]{1,2,0:T(8,128)}, f32[8,128,32]{1,2,0:T(8,128)}) async-done(((f32[8,128,4096]{1,2,0:T(8,128)}, f32[8,128,32]{1,2,0:T(8,128)}), (f32[8,128,4096]{1,2,0:T(8,128)}, f32[8,128,32]{1,2,0:T(8,128)})) %all-reduce.10.cloned.1.call-update) | async-done | bytes 16908304 | tf_op jit(solution)/shard_map/psum | solution.py:12
  1000.6 2.1 fusion.9
  1002.8 216.5 %all-reduce.8.cloned.1.call-done = (f32[8,128,4096]{1,2,0:T(8,128)}, f32[8,128,32]{1,2,0:T(8,128)}) async-done(((f32[8,128,4096]{1,2,0:T(8,128)}, f32[8,128,32]{1,2,0:T(8,128)}), (f32[8,128,4096]{1,2,0:T(8,128)}, f32[8,128,32]{1,2,0:T(8,128)})) %all-reduce.8.cloned.1.call-update) | async-done | bytes 16908304 | tf_op jit(solution)/shard_map/psum | solution.py:13
  1220.5 5.3 constant_dynamic-slice_fusion.3
  1225.8 2.8 copy.49
  (96 shorter events, 59.2 us)
Async XLA Ops:
  6.5 991.8 %copy-start = (bf16[1024,1024]{1,0:T(8,128)(2,1)S(1)}, bf16[1024,1024]{1,0:T(8,128)(2,1)}, u32[]{:S(2)}) copy-start(bf16[1024,1024]{1,0:T(8,128)(2,1)} %param.12) | copy-start | bytes 6291460
  6.5 33.1 %all-gather.3.cloned.1.call-start = ((), (), s32[]{:S(2)}) async-start(), calls=%async_computation | async-start | bytes 1310720 | tf_op jit(solution)/shard_map/all_gather | solution.py:55
  8.5 86.7 %all-gather.5.cloned.1.call-start = ((), (), s32[]{:S(2)}) async-start(), calls=%async_computation.1 | async-start | bytes 9437184 | tf_op jit(solution)/shard_map/all_gather | solution.py:56
  39.7 380.4 %all-reduce.6.cloned.1.call-start = ((), (), s32[]{:S(2)}) async-start(), calls=%async_computation.2 | async-start | bytes 262144 | tf_op jit(solution)/shard_map/pmax | solution.py:61
  39.8 67.9 %copy-start.4 = (s32[8]{0:T(128)S(1)}, s32[8]{0:T(128)}, u32[]{:S(2)}) copy-start(s32[8]{0:T(128)} %param.14) | copy-start | bytes 100
  115.9 3.2 copy-start.1
  139.3 3.2 copy-start.1
  162.7 3.2 copy-start.1
  186.2 3.2 copy-start.1
  209.6 3.2 copy-start.1
  233.1 3.2 copy-start.1
  256.6 3.2 copy-start.1
  280.0 3.2 copy-start.1
  295.3 703.0 %all-reduce.10.cloned.1.call-start = ((), (), s32[]{:S(2)}) async-start(), calls=%async_computation.4 | async-start | bytes 33816576 | tf_op jit(solution)/shard_map/psum | solution.py:12
  433.0 786.3 %all-reduce.8.cloned.1.call-start = ((), (), s32[]{:S(2)}) async-start(), calls=%async_computation.3 | async-start | bytes 33816576 | tf_op jit(solution)/shard_map/psum | solution.py:13
  998.3 0.7 copy-start.3
  998.3 1.3 copy-start.2
Sparse Core Ops, SparseCore 0:
  8.9 30.6 all-gather.2
  41.5 53.6 all-gather.4
  295.4 124.6 all-reduce.5
  433.2 565.1 all-reduce.9
  1002.2 217.0 all-reduce.7
